TPU v7x, 32 devices: a whole 2x2x4 slice. The times are simulated.
32 devices in a mesh: rep: 2 (over y), fsdp: 16 (over z, x, core).
Axes of the slice: x: 2, y: 2, z: 4, core: 2. Of those that a mesh axis runs over, the one named last changes fastest.
Arguments:
- tokens: bfloat16 [16384, 4096], P(('rep', 'fsdp')), may hold values from -6 to 6
- value_cot: bfloat16 [16384, 1024], P(('rep', 'fsdp')), may hold values from -6 to 6
- value_weight: bfloat16 [2, 4096, 1024], P('rep', 'fsdp'), may hold values from -0.09375 to 0.09375
- global_params: float32 [2097152], P('fsdp'), may hold values from -6 to 6
- local_params: float32 [2, 2097152], P('rep', 'fsdp'), may hold values from -6 to 6
- momentum: float32 [2097152], P('fsdp'), may hold values from -3 to 3
Outputs:
- token_grad: bfloat16 [16384, 4096], P(('rep', 'fsdp'))
- value_grad: float32 [2, 4096, 1024], P('rep', 'fsdp')
- new_global: float32 [2097152], P('fsdp')
- new_moment: float32 [2097152], P('fsdp')
All inputs are finite; a program needn't handle non-finite values.
Results may differ from a plain program's by a relative error of at most 0.001.
Values may be sent and summed in bfloat16 or wider, within the bound.
A program may use at most 128 MiB of HBM per device.

v0:
```python
import jax
import jax.numpy as jnp
from jax import lax
from jax.sharding import PartitionSpec as P


def grad_term(tokens, columns):
    return lax.dot_general(
        tokens, columns, (((0,), (0,)), ((), ())), preferred_element_type=jnp.float32
    )


def shards(tokens, value_cot, value_weight, global_params, local_params, momentum):
    weight = value_weight[0]
    token_grad = lax.dot_general(
        value_cot,
        lax.all_gather(weight, "fsdp", axis=0, tiled=True),
        (((1,), (1,)), ((), ())),
        preferred_element_type=jnp.float32,
    ).astype(jnp.bfloat16)
    groups = lax.axis_size("fsdp")
    factor = 1.0 / jnp.sqrt(jnp.float32(tokens.shape[0] * groups))
    summed = lax.psum_scatter(grad_term(tokens, value_cot), "fsdp", scatter_dimension=0, tiled=True)
    value_grad = (summed * factor)[None]
    totals = lax.psum(local_params[0], "rep")
    pseudo = global_params - totals / lax.axis_size("rep")
    new_moment = 0.9 * momentum + pseudo
    new_global = global_params - 0.7 * (pseudo + 0.9 * new_moment)
    return (token_grad, value_grad, new_global, new_moment)


def solution(mesh):
    in_specs = (
        P(("rep", "fsdp"), None),
        P(("rep", "fsdp"), None),
        P("rep", "fsdp", None),
        P("fsdp"),
        P("rep", "fsdp"),
        P("fsdp"),
    )
    out_specs = (P(("rep", "fsdp"), None), P("rep", "fsdp", None), P("fsdp"), P("fsdp"))
    return jax.shard_map(shards, mesh=mesh, in_specs=in_specs, out_specs=out_specs, check_vma=False)
```

profile of v0, /device:TPU:0, one launch (start us, length us, event | category | flops | bytes accessed | tf_op | source)
XLA Modules:
  0.0 277.8 jit_solution(12506146668002710478)
XLA Ops:
  8.0 0.0 copy-start
  8.0 0.0 all-reduce.2.cloned.1.call-start
  8.1 0.7 all-reduce.2.cloned.1.call-update
  8.7 0.0 all-gather.3.cloned.1.call-start
  8.8 0.5 all-gather.3.cloned.1.call-update
  9.3 0.0 reduce-scatter.2.cloned.1.call-start
  9.4 0.0 copy-done
  9.4 10.6 %fusion.5 = f32[4096,1024]{1,0:T(8,128)} fusion(bf16[512,4096]{1,0:T(8,128)(2,1)} %param.6, bf16[512,1024]{1,0:T(8,128)(2,1)S(1)} %copy-done), kind=kOutput, calls=%fused_computation.7 | convolution fusion | flops 4294967296 | bytes 22020096 | tf_op jit(solution)/shard_map/dot_general | solution.py:8
  20.0 0.0 copy-start.1
  20.0 0.0 copy-start.2
  20.0 0.0 reduce-scatter.2.cloned.1.call-update
  20.0 22.5 %all-reduce.2.cloned.1.call-done = f32[131072]{0:T(1024)} async-done(((f32[131072]{0:T(1024)}), f32[131072]{0:T(1024)}) %all-reduce.2.cloned.1.call-update) | async-done | bytes 524304 | tf_op jit(solution)/shard_map/psum | solution.py:25
  42.5 0.0 copy-done.1
  42.5 0.0 copy-done.2
  42.5 2.1 multiply_subtract_fusion
  44.7 43.5 %all-gather.3.cloned.1.call-done = bf16[1,4096,1024]{2,1,0:T(8,128)(2,1)} async-done(((bf16[1,256,1024]{2,1,0:T(8,128)(2,1)}), bf16[1,4096,1024]{2,1,0:T(8,128)(2,1)}) %all-gather.3.cloned.1.call-update) | async-done | bytes 8388624 | tf_op jit(solution)/shard_map/all_gather | solution.py:17
  88.2 9.5 %fusion.2 = bf16[512,4096]{1,0:T(8,128)(2,1)} fusion(bf16[512,1024]{1,0:T(8,128)(2,1)S(1)} %copy-done, bf16[1,4096,1024]{2,1,0:T(8,128)(2,1)} %all-gather.3.cloned.1.call-done), kind=kOutput, calls=%fused_computation.2 | convolution fusion | flops 4297064448 | bytes 13631488 | tf_op jit(solution)/shard_map/dot_general | solution.py:15
  97.7 170.4 %reduce-scatter.2.cloned.1.call-done = f32[256,1024]{1,0:T(8,128)} async-done(((f32[4096,1024]{1,0:T(8,128)}), f32[256,1024]{1,0:T(8,128)}) %reduce-scatter.2.cloned.1.call-update) | async-done | bytes 1048592 | tf_op jit(solution)/shard_map/reduce_scatter | solution.py:23
  268.0 2.3 multiply_bitcast_fusion
Async XLA Ops:
  8.0 1.4 copy-start
  8.0 34.5 %all-reduce.2.cloned.1.call-start = ((), (), s32[]{:S(2)}) async-start(), calls=%async_computation.2 | async-start | bytes 1048576 | tf_op jit(solution)/shard_map/psum | solution.py:25
  8.7 79.4 %all-gather.3.cloned.1.call-start = ((), (), s32[]{:S(2)}) async-start(), calls=%async_computation.3 | async-start | bytes 8912896 | tf_op jit(solution)/shard_map/all_gather | solution.py:17
  9.3 258.7 %reduce-scatter.2.cloned.1.call-start = ((), (), s32[]{:S(2)}) async-start(), calls=%async_computation.1 | async-start | bytes 17825792 | tf_op jit(solution)/shard_map/reduce_scatter | solution.py:23
  20.0 22.6 %copy-start.1 = (f32[131072]{0:T(1024)S(1)}, f32[131072]{0:T(1024)}, u32[]{:S(2)}) copy-start(f32[131072]{0:T(1024)} %param.9) | copy-start | bytes 1572868
  20.0 22.6 %copy-start.2 = (f32[131072]{0:T(1024)S(1)}, f32[131072]{0:T(1024)}, u32[]{:S(2)}) copy-start(f32[131072]{0:T(1024)} %param.11) | copy-start | bytes 1572868
Sparse Core Ops, SparseCore 0:
  11.1 31.3 all-reduce.1
Sparse Core Ops, SparseCore 1:
  11.4 76.7 all-gather.2
  92.2 175.8 reduce-scatter.1
where the time goes:
time: 278 us
  waiting for transfers between devices  238 us (86%)
  matrix products  20 us (7%)
  between operations  15.5 us (6%)
  other arithmetic  4.49 us (2%)
    reduce_scatter x1, waiting for transfers between devices, shards(): lax.psum_scatter(grad_term(tokens, value_cot), 'fsdp', scatter_dimension=...  170 us
    all_gather x1, waiting for transfers between devices, shards(): lax.all_gather(weight, 'fsdp', axis=0, tiled=True)  43.5 us
    psum x1, waiting for transfers between devices, shards(): totals = lax.psum(local_params[0], 'rep')  22.5 us
    dot_general x1, matrix products, grad_term(): lax.dot_general(tokens, columns, (((0,), (0,)), ((), ())), preferred_elem...  10.6 us
    dot_general x1, matrix products, shards(): lax.dot_general(value_cot, lax.all_gather(weight, 'fsdp', axis=0, tiled=T...  9.45 us
  transfers between devices with their start and end apart: 3, of which 3 were waited for; matrix products, arithmetic and copies ran while one was open for 8% of the time, Pallas kernels for 0%

commit v1 on v0

v1 whole, which is shorter than its diff:
```python
import functools

import jax
import jax.numpy as jnp
from jax import lax
from jax.experimental import pallas as pl
from jax.experimental.pallas import tpu as pltpu
from jax.sharding import PartitionSpec as P

CORES = 2
COLS = 2
SCALE = 2.0 ** 8


def grad_term(tokens, columns):
    return lax.dot_general(
        tokens, columns, (((0,), (0,)), ((), ())), preferred_element_type=jnp.float32
    )


def pack(v):
    v = v * SCALE
    v = v * jnp.abs(v)
    return (v * jnp.abs(v)).astype(jnp.bfloat16)


def unpack(p):
    p = p.astype(jnp.float32)
    r = jnp.sqrt(jnp.sqrt(jnp.abs(p))) * (1.0 / SCALE)
    return jnp.where(p < 0, -r, r)


def kernel(groups, factor, x_ref, c_ref, w_ref, tg_ref, vg_ref,
           wbuf, xr, cr, acc_a, acc_b, sax, rax, saz, raz, sbz, rbz, sbx, rbx,
           rw, szr, szl, sx, sc, xs, xrs, cs, own_sem, axs, axr, azs, azr, bzs, bzr, bxs):
    nz = groups // (CORES * COLS)
    f = lax.axis_index("fsdp")
    core, x, z = lax.rem(f, CORES), lax.rem(f // CORES, COLS), f // (CORES * COLS)
    depth = w_ref.shape[0]
    half = depth // 2
    wide = c_ref.shape[1] // 2

    def ident(zz, xx, cc):
        return (zz * COLS + xx) * CORES + cc

    ox, oc = 1 - x, 1 - core
    xdev, cdev = ident(z, ox, core), ident(z, x, oc)
    rdev, ldev = ident(z + 1, x, core), ident(z - 1, x, core)
    has_r, has_l = z < nz - 1, z > 0

    def both(fn):
        pl.when(has_r)(lambda: fn(rdev))
        pl.when(has_l)(lambda: fn(ldev))

    barrier = pltpu.get_barrier_semaphore()

    def greet(dev):
        pl.semaphore_signal(barrier, inc=1, device_id={"fsdp": dev}, device_id_type=pl.DeviceIdType.MESH)

    own = pltpu.make_async_copy(w_ref, wbuf.at[f], own_sem)
    own.start()
    greet(xdev)
    greet(cdev)
    both(greet)
    pl.semaphore_wait(barrier, 2 + jnp.where(has_r, 1, 0) + jnp.where(has_l, 1, 0))

    def remote(src, dst, ssem, rsem, dev):
        return pltpu.make_async_remote_copy(
            src_ref=src, dst_ref=dst, send_sem=ssem, recv_sem=rsem,
            device_id={"fsdp": dev}, device_id_type=pl.DeviceIdType.MESH)

    cot = remote(c_ref, cr, cs.at[0], cs.at[1], cdev)
    cot.start()

    def xcopy(q):
        d = q * CORES + oc
        return remote(x_ref.at[:, pl.ds(pl.multiple_of(d * depth, depth), depth)], xr.at[q], xs.at[q], xrs.at[q], cdev)

    nq = nz * COLS

    @pl.loop(0, nq)
    def _(q):
        xcopy(q).start()

    own.wait()

    def piece(h, blk, ssem, dev):
        part = wbuf.at[blk, pl.ds(h * half, half)]
        return remote(part, part, ssem.at[h, blk], rw.at[h, blk], dev)

    def right(h, blk):
        return piece(h, blk, szr, rdev)

    def left(h, blk):
        return piece(h, blk, szl, ldev)

    def across(h, blk):
        return piece(h, blk, sx, xdev)

    def core_way(h, blk):
        return piece(h, blk, sc, cdev)

    def send_z(h, blk):
        pl.when(has_r)(lambda: right(h, blk).start())
        pl.when(has_l)(lambda: left(h, blk).start())

    across(1, f).start()
    send_z(0, f)
    send_z(1, f)
    across(0, f).start()
    core_way(0, f).start()
    core_way(1, f).start()

    cot.wait_recv()

    @pl.loop(0, nq)
    def _(q):
        xcopy(q).wait_recv()

    def grad(zz, xx):
        q = zz * COLS + xx
        d = ident(zz, xx, core)
        cols = pl.ds(pl.multiple_of(d * depth, depth), depth)
        return grad_term(x_ref[:, cols], c_ref[...]) + grad_term(xr[q], cr[...])

    def ax(zz):
        return remote(sax.at[zz], rax.at[zz], axs.at[zz], axr.at[zz], xdev)

    @pl.loop(0, nz)
    def _(zz):
        g = grad(zz, ox)
        sax[zz] = pack(g[:, :wide])
        ax(zz).start()
        acc_b[zz, ox] = g[:, wide:]

    other = ident(z, ox, core)
    across(1, other).wait_recv()
    send_z(1, other)
    core_way(1, other).start()

    @pl.loop(0, nz)
    def _(zz):
        g = grad(zz, x)
        acc_a[zz] = g[:, :wide]
        acc_b[zz, x] = g[:, wide:]

    def hop(k):
        for h in range(2):
            for ok, zo, fwd, nxt in ((z - k >= 0, z - k, right, has_r), (z + k < nz, z + k, left, has_l)):
                @pl.when(ok)
                def _():
                    for xx in ((x,) if h == 0 else (x, ox)):
                        blk = ident(zo, xx, core)
                        fwd(h, blk).wait_recv()
                        pl.when(nxt)(lambda: fwd(h, blk).start())
                        if h == 0:
                            across(h, blk).start()
                        core_way(h, blk).start()

    def line(acc, sbuf, rbuf, ssem, rsem):
        def copy(way, zz):
            return remote(sbuf.at[zz], rbuf.at[way, zz], ssem.at[zz], rsem.at[way, zz], rdev if way == 0 else ldev)

        def step(j):
            for way, zz, more, mine, came in (
                (0, nz - 1 - j, nz - 1 - j > z, nz - 1 - j == z, has_l),
                (1, j, j < z, j == z, has_r),
            ):
                @pl.when(jnp.logical_and(jnp.logical_or(more, mine), came))
                def _():
                    copy(way, zz).wait_recv()
                    acc[zz] += unpack(rbuf[way, zz])

                @pl.when(more)
                def _():
                    sbuf[zz] = pack(acc[zz])
                    copy(way, zz).start()

        def drain():
            for zz in range(nz):
                pl.when(zz > z)(lambda: copy(0, zz).wait_send())
                pl.when(zz < z)(lambda: copy(1, zz).wait_send())

        return step, drain

    step_a, drain_a = line(acc_a, saz, raz, azs, azr)
    step_b, drain_b = line(acc_b, sbz, rbz, bzs, bzr)

    hop(1)
    step_b(0)
    hop(2) if nz > 2 else None

    @pl.loop(0, nz)
    def _(zz):
        ax(zz).wait_recv()
        acc_a[zz] += unpack(rax[zz])

    for j in range(1, nz):
        step_a(j - 1)
        if j + 2 < nz:
            hop(j + 2)
        step_b(j)
    bx = remote(sbx, rbx, bxs.at[0], bxs.at[1], xdev)
    sbx[...] = pack(acc_b[z, ox])
    bx.start()
    step_a(nz - 1)

    for zo in range(nz):
        blk = ident(zo, ox, core)
        across(0, blk).wait_recv()
        core_way(0, blk).start()

    def project(d):
        tg_ref[:, pl.ds(pl.multiple_of(d * depth, depth), depth)] = lax.dot_general(
            c_ref[...], wbuf[d], (((1,), (1,)), ((), ())), preferred_element_type=jnp.float32
        ).astype(jnp.bfloat16)

    @pl.loop(0, nq)
    def _(q):
        project(q * CORES + core)

    vg_ref[:, :wide] = acc_a[z] * factor
    bx.wait_recv()
    vg_ref[:, wide:] = (acc_b[z, x] + unpack(rbx[...])) * factor

    @pl.loop(0, nq)
    def _(q):
        d = q * CORES + oc
        core_way(0, d).wait_recv()
        core_way(1, d).wait_recv()
        project(d)

    cot.wait_send()
    bx.wait_send()
    drain_a()
    drain_b()

    @pl.loop(0, nq)
    def _(q):
        xcopy(q).wait_send()
        d = q * CORES + core
        core_way(0, d).wait_send()
        core_way(1, d).wait_send()

    across(1, f).wait_send()

    @pl.loop(0, nz)
    def _(zz):
        ax(zz).wait_send()
        across(0, ident(zz, x, core)).wait_send()
        go_r = jnp.logical_and(zz <= z, has_r)
        go_l = jnp.logical_and(zz >= z, has_l)
        for h, xx in ((0, x), (1, x), (1, ox)):
            pl.when(go_r)(lambda: right(h, ident(zz, xx, core)).wait_send())
            pl.when(go_l)(lambda: left(h, ident(zz, xx, core)).wait_send())


def fused(tokens, value_cot, weight, groups, factor):
    nz = groups // (CORES * COLS)
    rows, wide = tokens.shape[0], value_cot.shape[1]
    depth = weight.shape[0]
    w2 = wide // 2
    bf, f32 = jnp.bfloat16, jnp.float32
    dma = pltpu.SemaphoreType.DMA
    vmem = pl.BlockSpec(memory_space=pltpu.VMEM)
    return pl.pallas_call(
        functools.partial(kernel, groups, factor),
        out_shape=(
            jax.ShapeDtypeStruct((rows, tokens.shape[1]), bf),
            jax.ShapeDtypeStruct((depth, wide), f32),
        ),
        in_specs=[vmem] * 3,
        out_specs=(vmem, vmem),
        scratch_shapes=[
            pltpu.VMEM((groups, depth, wide), bf),
            pltpu.VMEM((nz * COLS, rows, depth), bf),
            pltpu.VMEM((rows, wide), bf),
            pltpu.VMEM((nz, depth, w2), f32),
            pltpu.VMEM((nz, COLS, depth, w2), f32),
            pltpu.VMEM((nz, depth, w2), bf),
            pltpu.VMEM((nz, depth, w2), bf),
            pltpu.VMEM((nz, depth, w2), bf),
            pltpu.VMEM((2, nz, depth, w2), bf),
            pltpu.VMEM((nz, COLS, depth, w2), bf),
            pltpu.VMEM((2, nz, COLS, depth, w2), bf),
            pltpu.VMEM((depth, w2), bf),
            pltpu.VMEM((depth, w2), bf),
            dma((2, groups)), dma((2, groups)), dma((2, groups)), dma((2, groups)), dma((2, groups)),
            dma((nz * COLS,)), dma((nz * COLS,)), dma((2,)), dma,
            dma((nz,)), dma((nz,)), dma((nz,)), dma((2, nz)), dma((nz,)), dma((2, nz)), dma((2,)),
        ],
        compiler_params=pltpu.CompilerParams(
            collective_id=0, has_side_effects=True, vmem_limit_bytes=56 * 1024 * 1024
        ),
        cost_estimate=pl.CostEstimate(flops=80_000_000_000, bytes_accessed=20_000_000, transcendentals=0),
    )(tokens, value_cot, weight)


def shards(tokens, value_cot, value_weight, global_params, local_params, momentum):
    weight = value_weight[0]
    groups = lax.axis_size("fsdp")
    reps = lax.axis_size("rep")
    local = local_params[0]
    factor = 1.0 / float(tokens.shape[0] * groups) ** 0.5
    if reps == 2:
        totals = local + lax.ppermute(local, "rep", [(0, 1), (1, 0)])
    else:
        totals = lax.psum(local, "rep")
    depth = weight.shape[0]
    if depth % 128 == 0 and groups % (CORES * COLS) == 0 and groups > CORES * COLS:
        token_grad, value_grad = fused(tokens, value_cot, weight, groups, factor)
    else:
        token_grad = lax.dot_general(
            value_cot,
            lax.all_gather(weight, "fsdp", axis=0, tiled=True),
            (((1,), (1,)), ((), ())),
            preferred_element_type=jnp.float32,
        ).astype(jnp.bfloat16)
        value_grad = factor * lax.psum_scatter(
            grad_term(tokens, value_cot), "fsdp", scatter_dimension=0, tiled=True
        )
    pseudo = global_params - totals / reps
    new_moment = 0.9 * momentum + pseudo
    new_global = global_params - 0.7 * (pseudo + 0.9 * new_moment)
    return (token_grad, value_grad[None], new_global, new_moment)


def solution(mesh):
    in_specs = (
        P(("rep", "fsdp"), None),
        P(("rep", "fsdp"), None),
        P("rep", "fsdp", None),
        P("fsdp"),
        P("rep", "fsdp"),
        P("fsdp"),
    )
    out_specs = (P(("rep", "fsdp"), None), P("rep", "fsdp", None), P("fsdp"), P("fsdp"))
    return jax.shard_map(shards, mesh=mesh, in_specs=in_specs, out_specs=out_specs, check_vma=False)
```

time: 278 us -> 211 us (0.76)
  the two profiles are of different devices: /device:TPU:0 before, /device:TPU:8 now
where the time goes in v1:
time: 211 us
  Pallas kernels  202 us (96%)
  local copies, waits for them, and re-layouts  5.77 us (3%)
    pallas_call x1, Pallas kernels, fused(): pl.pallas_call(functools.partial(kernel, groups, factor), out_shape=(jax....  202 us
    unnamed x10, local copies, waits for them, and re-layouts  5.77 us
  transfers between devices with their start and end apart: 1, of which 0 were waited for; matrix products, arithmetic and copies ran while one was open for 0% of the time, Pallas kernels for 96%

profile of v1, /device:TPU:8, one launch (start us, length us, event | category | flops | bytes accessed | tf_op | source)
XLA Modules:
  0.0 210.7 jit_solution(18116224468473348559)
XLA Ops:
  0.6 1.6 collective-permute-start
  2.2 0.0 copy-start.1
  2.2 0.0 copy-start.2
  2.2 0.0 copy-start.3
  2.2 201.5 %shard_map.93 = (bf16[512,4096]{1,0:T(8,128)(2,1)}, f32[256,1024]{1,0:T(8,128)}) custom-call(bf16[512,4096]{1,0:T(8,128)(2,1)} %x_ref.1, bf16[512,1024]{1,0:T(8,128)(2,1)} %c_ref.1, bf16[256,1024]{1,0:T(8,128)(2,1)} %bitcast.6), custom_call_target="tpu_custom_call" | custom-call | flops 80000000000 | bytes 20000000 | tf_op jit(solution)/shard_map/pallas_call | solution.py:266
  203.8 0.0 collective-permute-done
  203.8 0.0 copy-done.1
  203.8 0.0 copy-done.2
  203.8 0.0 copy-done.3
  203.8 1.1 multiply_subtract_fusion
  204.9 0.0 copy-start
  204.9 4.8 %copy.12 = bf16[512,4096]{1,0:T(8,128)(2,1)} copy(bf16[512,4096]{1,0:T(8,128)(2,1)} %get-tuple-element.14) | data formatting | bytes 8388608
  209.7 0.0 copy-done
  209.7 1.0 copy.13
Async XLA Ops:
  0.6 203.1 %collective-permute-start = (f32[131072]{0:T(1024)}, f32[131072]{0:T(1024)S(1)}, u32[]{:S(2)}, u32[]{:S(2)}) collective-permute-start(f32[131072]{0:T(1024)} %bitcast.4), channel_id=1, source_target_pairs={{0,16},{16,0},{1,17},{17,1},{2,18},{18,2},{3,19},{19,3},{4,20},{20... | collective-permute-start | bytes 1572872 | tf_op jit(solution)/shard_map/ppermute | solution.py:306
  2.2 201.6 %copy-start.1 = (f32[131072]{0:T(1024)S(1)}, f32[131072]{0:T(1024)}, u32[]{:S(2)}) copy-start(f32[131072]{0:T(1024)} %param.9) | copy-start | bytes 1572868
  2.2 201.6 %copy-start.2 = (f32[1,131072]{1,0:T(1,128)S(1)}, f32[1,131072]{1,0:T(1,128)}, u32[]{:S(2)}) copy-start(f32[1,131072]{1,0:T(1,128)} %param.10) | copy-start | bytes 1572868
  2.2 201.6 %copy-start.3 = (f32[131072]{0:T(1024)S(1)}, f32[131072]{0:T(1024)}, u32[]{:S(2)}) copy-start(f32[131072]{0:T(1024)} %param.11) | copy-start | bytes 1572868
  204.9 4.8 %copy-start = (f32[256,1024]{1,0:T(8,128)S(1)}, f32[256,1024]{1,0:T(8,128)}, u32[]{:S(2)}) copy-start(f32[256,1024]{1,0:T(8,128)} %get-tuple-element.7) | copy-start | bytes 3145732

commit v2 on v1

--- a/solution.py
+++ b/solution.py
@@ -107,7 +107,6 @@
     across(1, f).start()
     send_z(0, f)
     send_z(1, f)
-    across(0, f).start()
     core_way(0, f).start()
     core_way(1, f).start()
 
@@ -132,6 +131,8 @@
         sax[zz] = pack(g[:, :wide])
         ax(zz).start()
         acc_b[zz, ox] = g[:, wide:]
+
+    across(0, f).start()
 
     other = ident(z, ox, core)
     across(1, other).wait_recv()
@@ -161,20 +162,19 @@
         def copy(way, zz):
             return remote(sbuf.at[zz], rbuf.at[way, zz], ssem.at[zz], rsem.at[way, zz], rdev if way == 0 else ldev)
 
-        def step(j):
-            for way, zz, more, mine, came in (
-                (0, nz - 1 - j, nz - 1 - j > z, nz - 1 - j == z, has_l),
-                (1, j, j < z, j == z, has_r),
-            ):
-                @pl.when(jnp.logical_and(jnp.logical_or(more, mine), came))
+        def step(s):
+            late = nz - 1 - s
+            for way, zz, ok, came in ((0, z + late, z <= s, has_l), (1, z - late, nz - 1 - z <= s, has_r)):
+                @pl.when(jnp.logical_and(ok, came))
                 def _():
                     copy(way, zz).wait_recv()
                     acc[zz] += unpack(rbuf[way, zz])
 
-                @pl.when(more)
-                def _():
-                    sbuf[zz] = pack(acc[zz])
-                    copy(way, zz).start()
+                if late:
+                    @pl.when(ok)
+                    def _():
+                        sbuf[zz] = pack(acc[zz])
+                        copy(way, zz).start()
 
         def drain():
             for zz in range(nz):
@@ -186,24 +186,20 @@
     step_a, drain_a = line(acc_a, saz, raz, azs, azr)
     step_b, drain_b = line(acc_b, sbz, rbz, bzs, bzr)
 
-    hop(1)
     step_b(0)
-    hop(2) if nz > 2 else None
-
-    @pl.loop(0, nz)
-    def _(zz):
-        ax(zz).wait_recv()
-        acc_a[zz] += unpack(rax[zz])
-
-    for j in range(1, nz):
-        step_a(j - 1)
-        if j + 2 < nz:
-            hop(j + 2)
-        step_b(j)
-    bx = remote(sbx, rbx, bxs.at[0], bxs.at[1], xdev)
-    sbx[...] = pack(acc_b[z, ox])
-    bx.start()
-    step_a(nz - 1)
+    for s in range(1, nz):
+        hop(s)
+        step_b(s)
+        if s == 1:
+            @pl.loop(0, nz)
+            def _(zz):
+                ax(zz).wait_recv()
+                acc_a[zz] += unpack(rax[zz])
+        if s == nz - 1:
+            bx = remote(sbx, rbx, bxs.at[0], bxs.at[1], xdev)
+            sbx[...] = pack(acc_b[z, ox])
+            bx.start()
+        step_a(s - 1)
 
     for zo in range(nz):
         blk = ident(zo, ox, core)
@@ -219,6 +215,7 @@
     def _(q):
         project(q * CORES + core)
 
+    step_a(nz - 1)
     vg_ref[:, :wide] = acc_a[z] * factor
     bx.wait_recv()
     vg_ref[:, wide:] = (acc_b[z, x] + unpack(rbx[...])) * factor

time: 211 us -> 96.2 us (0.46)
  the two profiles are of different devices: /device:TPU:8 before, /device:TPU:0 now
where the time goes in v2:
time: 96.2 us; the launch traced here: 96.1 us
  Pallas kernels  85.5 us (89%)
  local copies, waits for them, and re-layouts  5.77 us (6%)
  starting transfers between devices  3.06 us (3%)
  other arithmetic  1.12 us (1%)
    pallas_call x1, Pallas kernels, fused(): pl.pallas_call(functools.partial(kernel, groups, factor), out_shape=(jax....  85.5 us
    unnamed x10, local copies, waits for them, and re-layouts  5.77 us
    ppermute x1, starting transfers between devices, shards(): totals = local + lax.ppermute(local, 'rep', [(0, 1), (1, 0)])  3.06 us
  transfers between devices with their start and end apart: 1, of which 0 were waited for; matrix products, arithmetic and copies ran while one was open for 0% of the time, Pallas kernels for 89%

profile of v2, /device:TPU:0, one launch (start us, length us, event | category | flops | bytes accessed | tf_op | source)
XLA Modules:
  0.0 96.1 jit_solution(12248038745375742664)
XLA Ops:
  0.6 3.1 %collective-permute-start = (f32[131072]{0:T(1024)}, f32[131072]{0:T(1024)S(1)}, u32[]{:S(2)}, u32[]{:S(2)}) collective-permute-start(f32[131072]{0:T(1024)} %bitcast.4), channel_id=1, source_target_pairs={{0,16},{16,0},{1,17},{17,1},{2,18},{18,2},{3,19},{19,3},{4,20},{20... | collective-permute-start | bytes 1572872 | tf_op jit(solution)/shard_map/ppermute | solution.py:303
  3.7 0.0 copy-start.1
  3.7 0.0 copy-start.2
  3.7 0.0 copy-start.3
  3.7 85.5 %shard_map.93 = (bf16[512,4096]{1,0:T(8,128)(2,1)}, f32[256,1024]{1,0:T(8,128)}) custom-call(bf16[512,4096]{1,0:T(8,128)(2,1)} %x_ref.1, bf16[512,1024]{1,0:T(8,128)(2,1)} %c_ref.1, bf16[256,1024]{1,0:T(8,128)(2,1)} %bitcast.6), custom_call_target="tpu_custom_call" | custom-call | flops 80000000000 | bytes 20000000 | tf_op jit(solution)/shard_map/pallas_call | solution.py:263
  89.2 0.0 collective-permute-done
  89.2 0.0 copy-done.1
  89.2 0.0 copy-done.2
  89.2 0.0 copy-done.3
  89.2 1.1 %multiply_subtract_fusion = (f32[131072]{0:T(1024)}, f32[131072]{0:T(1024)}) fusion(f32[131072]{0:T(1024)S(1)} %copy-done.1, f32[131072]{0:T(1024)S(1)} %bitcast.5, f32[131072]{0:T(1024)S(1)} %collective-permute-done, f32[131072]{0:T(1024)S(1)} %copy-done.3), kind=kLoop, calls=%fused_computation | loop fusion | flops 1179648 | bytes 3145728 | tf_op jit(solution)/shard_map/sub | solution.py:321
  90.3 0.0 copy-start
  90.3 4.8 %copy.12 = bf16[512,4096]{1,0:T(8,128)(2,1)} copy(bf16[512,4096]{1,0:T(8,128)(2,1)} %get-tuple-element.14) | data formatting | bytes 8388608
  95.1 0.0 copy-done
  95.1 1.0 %copy.13 = f32[1,256,1024]{2,1,0:T(8,128)} copy(f32[1,256,1024]{2,1,0:T(8,128)S(1)} %bitcast.3) | data formatting | bytes 2097152
Async XLA Ops:
  0.6 88.5 %collective-permute-start = (f32[131072]{0:T(1024)}, f32[131072]{0:T(1024)S(1)}, u32[]{:S(2)}, u32[]{:S(2)}) collective-permute-start(f32[131072]{0:T(1024)} %bitcast.4), channel_id=1, source_target_pairs={{0,16},{16,0},{1,17},{17,1},{2,18},{18,2},{3,19},{19,3},{4,20},{20... | collective-permute-start | bytes 1572872 | tf_op jit(solution)/shard_map/ppermute | solution.py:303
  3.7 85.5 %copy-start.1 = (f32[131072]{0:T(1024)S(1)}, f32[131072]{0:T(1024)}, u32[]{:S(2)}) copy-start(f32[131072]{0:T(1024)} %param.9) | copy-start | bytes 1572868
  3.7 85.5 %copy-start.2 = (f32[1,131072]{1,0:T(1,128)S(1)}, f32[1,131072]{1,0:T(1,128)}, u32[]{:S(2)}) copy-start(f32[1,131072]{1,0:T(1,128)} %param.10) | copy-start | bytes 1572868
  3.7 85.5 %copy-start.3 = (f32[131072]{0:T(1024)S(1)}, f32[131072]{0:T(1024)}, u32[]{:S(2)}) copy-start(f32[131072]{0:T(1024)} %param.11) | copy-start | bytes 1572868
  90.3 4.8 %copy-start = (f32[256,1024]{1,0:T(8,128)S(1)}, f32[256,1024]{1,0:T(8,128)}, u32[]{:S(2)}) copy-start(f32[256,1024]{1,0:T(8,128)} %get-tuple-element.7) | copy-start | bytes 3145732
